TPU v7x, 32 devices: a whole 2x2x4 slice. The times are simulated.
32 devices in a mesh: seq: 8 (over z, x), tp: 4 (over y, core).
Axes of the slice: x: 2, y: 2, z: 4, core: 2. Of those that a mesh axis runs over, the one named last changes fastest.
Arguments:
- inputs: bfloat16 [2, 2048, 2048], P(None, 'seq'), may hold values from -6 to 6
- cotangent: bfloat16 [2, 2048, 2048], P(None, 'seq'), may hold values from -6 to 6
- attn_gain: bfloat16 [2048], P('seq'), may hold values from 0.5 to 1.5
- w_query: bfloat16 [2048, 2048], P('seq', 'tp'), may hold values from -0.125 to 0.125
- w_key: bfloat16 [2048, 2048], P('seq', 'tp'), may hold values from -0.125 to 0.125
- w_value: bfloat16 [2048, 3456], P('seq', 'tp'), may hold values from -0.125 to 0.125
- w_gate: bfloat16 [2048, 3456], P('seq', 'tp'), may hold values from -0.125 to 0.125
- w_out: bfloat16 [3456, 2048], P('tp', 'seq'), may hold values from -0.15625 to 0.15625
- ffn_gain: bfloat16 [2048], P('seq'), may hold values from 0.5 to 1.5
- w_glu: bfloat16 [2048, 3456], P('seq', 'tp'), may hold values from -0.125 to 0.125
- w_up: bfloat16 [2048, 3456], P('seq', 'tp'), may hold values from -0.125 to 0.125
- w_down: bfloat16 [3456, 2048], P('tp', 'seq'), may hold values from -0.15625 to 0.15625
- decay_rate: float32 [8], P('tp'), may hold values from 0 to 0.032, as said below
Outputs:
- outputs: bfloat16 [2, 2048, 2048], P(None, 'seq')
- input_grad: float32 [2, 2048, 2048], P(None, 'seq')
- attngain_grad: float32 [2048], P('seq')
- query_grad: float32 [2048, 2048], P('seq', 'tp')
- key_grad: float32 [2048, 2048], P('seq', 'tp')
- value_grad: float32 [2048, 3456], P('seq', 'tp')
- gate_grad: float32 [2048, 3456], P('seq', 'tp')
- out_grad: float32 [3456, 2048], P('tp', 'seq')
- ffngain_grad: float32 [2048], P('seq')
- glu_grad: float32 [2048, 3456], P('seq', 'tp')
- up_grad: float32 [2048, 3456], P('seq', 'tp')
- down_grad: float32 [3456, 2048], P('tp', 'seq')
Inputs may be any that keep to these rules, and one draw needn't show every extreme that they name: `decay_rate`: each head's decay rate; positive.
All inputs are finite; a program needn't handle non-finite values.
Results may differ from a plain program's by a relative error of at most 0.03.
Values may be sent and summed in bfloat16 or wider, within the bound.
A program may use at most 256 MiB of HBM per device.

v0:
```python
import math
import jax
import jax.numpy as jnp
from jax import lax
from jax.sharding import PartitionSpec as P

KEY = 256
VAL = 432
EPS_LAYER = 1e-05
EPS_GROUP = 1e-06
MAXIMAL_ACCURACY = lax.Precision.HIGHEST


def passed_along(block, axis, distance):
    devices = range(lax.axis_size(axis))
    route = [(i - distance, i) for i in devices if i - distance in devices]
    return lax.ppermute(block, axis, route)


def normalize(values, epsilon):
    average = jnp.mean(values, axis=-1, keepdims=True)
    centred = values - average
    inv_std = lax.rsqrt(jnp.mean(centred * centred, axis=-1, keepdims=True) + epsilon)
    return (centred * inv_std, inv_std)


def normalize_back(upstream, normed, inv_std):
    return inv_std * (
        upstream
        - jnp.mean(upstream, axis=-1, keepdims=True)
        - normed * jnp.mean(upstream * normed, axis=-1, keepdims=True)
    )


def swish_parts(values):
    sigmoid = jax.nn.sigmoid(values)
    return (values * sigmoid, sigmoid * (1.0 + values * (1.0 - sigmoid)))


def rotary_tables(positions, width):
    half_width = width // 2
    fraction = jnp.arange(half_width, dtype=jnp.float32) / max(half_width - 1, 1)
    frequency = jnp.power(10000.0, -fraction)
    angles = positions[:, None] * frequency[None, :]
    cosine = jnp.concatenate([jnp.cos(angles), jnp.cos(angles)], axis=-1)[:, None, :]
    sine_table = jnp.concatenate([jnp.sin(angles), jnp.sin(angles)], axis=-1)[:, None, :]
    return (cosine, sine_table)


def rotate(values, cosine, sine_table):
    half_width = values.shape[-1] // 2
    turned = jnp.concatenate([-values[..., half_width:], values[..., :half_width]], axis=-1)
    return values * cosine + turned * sine_table


def rotate_back(upstream, cosine, sine_table):
    half_width = upstream.shape[-1] // 2
    scaled = upstream * sine_table
    turned = jnp.concatenate([scaled[..., half_width:], -scaled[..., :half_width]], axis=-1)
    return upstream * cosine + turned


def decay_tables(rates, length):
    offsets = jnp.arange(length, dtype=jnp.float32)
    distance = offsets[:, None] - offsets[None, :]
    decay_mask = jnp.where(
        distance[None] >= 0.0,
        jnp.exp(-rates[:, None, None] * jnp.maximum(distance, 0.0)[None]),
        0.0,
    )
    leading_decay = jnp.exp(-rates[None, :] * (offsets[:, None] + 1.0))
    trailing_decay = jnp.exp(-rates[None, :] * (length - 1.0 - offsets[:, None]))
    return (decay_mask, leading_decay, trailing_decay)


def block_summary(key_rotated, value_matrix_rows, trailing_decay):
    return jnp.einsum(
        "ysu,ysb->sub",
        key_rotated.astype(jnp.float32) * trailing_decay[:, :, None],
        value_matrix_rows.astype(jnp.float32),
        precision=MAXIMAL_ACCURACY,
    )


def block_weights(query_rotated, key_rotated, decay_mask):
    scores = jnp.einsum(
        "ihk,jhk->hij", query_rotated, key_rotated, preferred_element_type=jnp.float32
    )
    return (scores * decay_mask).astype(jnp.bfloat16)


def block_output(
    query_rotated, key_rotated, value_matrix_rows, incoming_state, decay_mask, leading_decay
):
    layer_weights = block_weights(query_rotated, key_rotated, decay_mask)
    inner = jnp.einsum(
        "hij,jhv->ihv", layer_weights, value_matrix_rows, preferred_element_type=jnp.float32
    )
    carried_state = jnp.einsum(
        "jnq,nqs->jns",
        query_rotated.astype(jnp.float32) * leading_decay[:, :, None],
        incoming_state,
        precision=MAXIMAL_ACCURACY,
    )
    return inner + carried_state


def state_grad_own(query_rotated, output_gradient, leading_decay):
    return jnp.einsum(
        "pxa,pxb->xab",
        query_rotated.astype(jnp.float32) * leading_decay[:, :, None],
        output_gradient.astype(jnp.float32),
        precision=MAXIMAL_ACCURACY,
    )


def block_backward(
    query_rotated,
    key_rotated,
    value_matrix_rows,
    incoming_state,
    state_gradient,
    output_gradient,
    decay_mask,
    leading_decay,
    trailing_decay,
):
    weight_gradients = (
        jnp.einsum(
            "ihv,jhv->hij", output_gradient, value_matrix_rows, preferred_element_type=jnp.float32
        )
        * decay_mask
    ).astype(jnp.bfloat16)
    layer_weights = block_weights(query_rotated, key_rotated, decay_mask)
    query_gradient = jnp.einsum(
        "pzg,gpe->zpe", weight_gradients, key_rotated, preferred_element_type=jnp.float32
    ) + leading_decay[:, :, None] * jnp.einsum(
        "wcr,cdr->wcd",
        output_gradient.astype(jnp.float32),
        incoming_state,
        precision=MAXIMAL_ACCURACY,
    )
    key_gradient = jnp.einsum(
        "zun,uzf->nzf", weight_gradients, query_rotated, preferred_element_type=jnp.float32
    ) + trailing_decay[:, :, None] * jnp.einsum(
        "crp,rnp->crn",
        value_matrix_rows.astype(jnp.float32),
        state_gradient,
        precision=MAXIMAL_ACCURACY,
    )
    value_gradient = jnp.einsum(
        "lpb,plz->blz", layer_weights, output_gradient, preferred_element_type=jnp.float32
    ) + trailing_decay[:, :, None] * jnp.einsum(
        "zmf,mfn->zmn", key_rotated.astype(jnp.float32), state_gradient, precision=MAXIMAL_ACCURACY
    )
    return (query_gradient, key_gradient, value_gradient)


def carry_states(whole_decay, summary):

    def advance(turn_index, carried_state):
        return passed_along(whole_decay * carried_state + summary, "seq", 1)

    return lax.fori_loop(0, lax.axis_size("seq") - 1, advance, jnp.zeros_like(summary))


def carry_back(whole_decay, own_grad):

    def retreat(turn_index, carried_state):
        return passed_along(whole_decay * carried_state + own_grad, "seq", -1)

    return lax.fori_loop(0, lax.axis_size("seq") - 1, retreat, jnp.zeros_like(own_grad))


def on_device(
    inputs,
    cotangent,
    attn_gain,
    w_query,
    w_key,
    w_value,
    w_gate,
    w_out,
    ffn_gain,
    w_glu,
    w_up,
    w_down,
    decay_rate,
):
    seq_count, tok_rows, model_width = inputs.shape
    row_count = seq_count * tok_rows
    local_heads = decay_rate.shape[0]
    gathered = (
        lax.all_gather(w_query, "seq", axis=0, tiled=True),
        lax.all_gather(w_key, "seq", axis=0, tiled=True),
        lax.all_gather(w_value, "seq", axis=0, tiled=True),
        lax.all_gather(w_gate, "seq", axis=0, tiled=True),
        lax.all_gather(w_out, "seq", axis=1, tiled=True),
        lax.all_gather(w_glu, "seq", axis=0, tiled=True),
        lax.all_gather(w_up, "seq", axis=0, tiled=True),
        lax.all_gather(w_down, "seq", axis=1, tiled=True),
        lax.all_gather(attn_gain, "seq", axis=0, tiled=True),
        lax.all_gather(ffn_gain, "seq", axis=0, tiled=True),
    )
    (
        full_query,
        full_key,
        full_value,
        full_gate,
        full_out,
        full_glu,
        full_up,
        full_down,
        full_attn_gain,
        full_ffn_gain,
    ) = gathered
    residual = inputs.astype(jnp.float32).reshape(row_count, model_width)
    normed_one, inv_one = normalize(residual, EPS_LAYER)
    attn_in = (normed_one * full_attn_gain.astype(jnp.float32)).astype(jnp.bfloat16)
    query_lin = jnp.dot(attn_in, full_query, preferred_element_type=jnp.float32)
    key_lin = jnp.dot(attn_in, full_key, preferred_element_type=jnp.float32)
    value_lin = jnp.dot(attn_in, full_value, preferred_element_type=jnp.float32)
    gate_lin = jnp.dot(attn_in, full_gate, preferred_element_type=jnp.float32)
    offset = (lax.axis_index("seq") * tok_rows).astype(jnp.float32)
    positions = offset + jnp.arange(tok_rows, dtype=jnp.float32)
    cosine, sine_table = rotary_tables(positions, KEY)
    key_scale = 1.0 / math.sqrt(KEY)
    query_rotated = rotate(
        query_lin.reshape(seq_count, tok_rows, local_heads, KEY), cosine, sine_table
    ).astype(jnp.bfloat16)
    key_rotated = (
        rotate(key_lin.reshape(seq_count, tok_rows, local_heads, KEY), cosine, sine_table)
        * key_scale
    ).astype(jnp.bfloat16)
    value_matrix_rows = value_lin.reshape(seq_count, tok_rows, local_heads, VAL).astype(
        jnp.bfloat16
    )
    decay_mask, leading_decay, trailing_decay = decay_tables(decay_rate, tok_rows)
    whole_decay = jnp.exp(-decay_rate * tok_rows)[:, None, None]
    summary = jax.vmap(block_summary, in_axes=(0, 0, None))(
        key_rotated, value_matrix_rows, trailing_decay
    )
    incoming_state = carry_states(whole_decay, summary)
    retained = jax.vmap(block_output, in_axes=(0, 0, 0, 0, None, None))(
        query_rotated, key_rotated, value_matrix_rows, incoming_state, decay_mask, leading_decay
    )
    group_normed, group_inv = normalize(retained, EPS_GROUP)
    gate_act, gate_slope = swish_parts(gate_lin)
    group_flat = group_normed.reshape(row_count, local_heads * VAL)
    mixed = (gate_act * group_flat).astype(jnp.bfloat16)
    attn_out = lax.psum(jnp.dot(mixed, full_out, preferred_element_type=jnp.float32), "tp")
    middle = residual + attn_out
    normed_two, inv_two = normalize(middle, EPS_LAYER)
    ffn_in = (normed_two * full_ffn_gain.astype(jnp.float32)).astype(jnp.bfloat16)
    glu_lin = jnp.dot(ffn_in, full_glu, preferred_element_type=jnp.float32)
    up_lin = jnp.dot(ffn_in, full_up, preferred_element_type=jnp.float32)
    glu_act, glu_slope = swish_parts(glu_lin)
    hidden = (glu_act * up_lin).astype(jnp.bfloat16)
    ffn_out = lax.psum(jnp.dot(hidden, full_down, preferred_element_type=jnp.float32), "tp")
    final = middle + ffn_out
    outputs = final.astype(jnp.bfloat16).reshape(seq_count, tok_rows, model_width)
    back_weights = (
        lax.all_gather(w_query, "seq", axis=0, tiled=True),
        lax.all_gather(w_key, "seq", axis=0, tiled=True),
        lax.all_gather(w_value, "seq", axis=0, tiled=True),
        lax.all_gather(w_gate, "seq", axis=0, tiled=True),
        lax.all_gather(w_out, "seq", axis=1, tiled=True),
        lax.all_gather(w_glu, "seq", axis=0, tiled=True),
        lax.all_gather(w_up, "seq", axis=0, tiled=True),
        lax.all_gather(w_down, "seq", axis=1, tiled=True),
        lax.all_gather(attn_gain, "seq", axis=0, tiled=True),
        lax.all_gather(ffn_gain, "seq", axis=0, tiled=True),
    )
    (
        back_query,
        back_key,
        back_value,
        back_gate,
        back_out,
        back_glu,
        back_up,
        back_down,
        back_attn_gain,
        back_ffn_gain,
    ) = back_weights
    cot_rows = cotangent.reshape(row_count, model_width)
    down_grad = jnp.dot(hidden.T, cot_rows, preferred_element_type=jnp.float32)
    grad_hidden = jnp.dot(cot_rows, back_down.T, preferred_element_type=jnp.float32)
    grad_glu = (grad_hidden * up_lin * glu_slope).astype(jnp.bfloat16)
    grad_up = (grad_hidden * glu_act).astype(jnp.bfloat16)
    glu_grad = jnp.dot(ffn_in.T, grad_glu, preferred_element_type=jnp.float32)
    up_grad = jnp.dot(ffn_in.T, grad_up, preferred_element_type=jnp.float32)
    grad_ffn_in = lax.psum(
        jnp.dot(grad_glu, back_glu.T, preferred_element_type=jnp.float32)
        + jnp.dot(grad_up, back_up.T, preferred_element_type=jnp.float32),
        "tp",
    )
    ffngain_grad = jnp.sum(grad_ffn_in * normed_two, axis=0)
    grad_middle = cot_rows.astype(jnp.float32) + normalize_back(
        grad_ffn_in * back_ffn_gain.astype(jnp.float32), normed_two, inv_two
    )
    grad_middle_bf = grad_middle.astype(jnp.bfloat16)
    out_grad = jnp.dot(mixed.T, grad_middle_bf, preferred_element_type=jnp.float32)
    grad_mixed = jnp.dot(grad_middle_bf, back_out.T, preferred_element_type=jnp.float32)
    grad_gate = (grad_mixed * group_flat * gate_slope).astype(jnp.bfloat16)
    grad_group = (grad_mixed * gate_act).reshape(seq_count, tok_rows, local_heads, VAL)
    grad_retained = normalize_back(grad_group, group_normed, group_inv).astype(jnp.bfloat16)
    own_grad = jax.vmap(state_grad_own, in_axes=(0, 0, None))(
        query_rotated, grad_retained, leading_decay
    )
    state_gradient = carry_back(whole_decay, own_grad)
    grad_qrot, grad_krot, grad_vrows = jax.vmap(
        block_backward, in_axes=(0, 0, 0, 0, 0, 0, None, None, None)
    )(
        query_rotated,
        key_rotated,
        value_matrix_rows,
        incoming_state,
        state_gradient,
        grad_retained,
        decay_mask,
        leading_decay,
        trailing_decay,
    )
    query_gradient = (
        rotate_back(grad_qrot, cosine, sine_table)
        .reshape(row_count, local_heads * KEY)
        .astype(jnp.bfloat16)
    )
    key_gradient = (
        (rotate_back(grad_krot, cosine, sine_table) * key_scale)
        .reshape(row_count, local_heads * KEY)
        .astype(jnp.bfloat16)
    )
    value_gradient = grad_vrows.reshape(row_count, local_heads * VAL).astype(jnp.bfloat16)
    query_grad = jnp.dot(attn_in.T, query_gradient, preferred_element_type=jnp.float32)
    key_grad = jnp.dot(attn_in.T, key_gradient, preferred_element_type=jnp.float32)
    value_grad = jnp.dot(attn_in.T, value_gradient, preferred_element_type=jnp.float32)
    gate_grad = jnp.dot(attn_in.T, grad_gate, preferred_element_type=jnp.float32)
    partial_in = (
        jnp.dot(query_gradient, back_query.T, preferred_element_type=jnp.float32)
        + jnp.dot(key_gradient, back_key.T, preferred_element_type=jnp.float32)
        + jnp.dot(value_gradient, back_value.T, preferred_element_type=jnp.float32)
        + jnp.dot(grad_gate, back_gate.T, preferred_element_type=jnp.float32)
    )
    grad_attn_in = lax.psum(partial_in, "tp")
    attngain_grad = jnp.sum(grad_attn_in * normed_one, axis=0)
    input_grad = grad_middle + normalize_back(
        grad_attn_in * back_attn_gain.astype(jnp.float32), normed_one, inv_one
    )
    input_out = input_grad.reshape(seq_count, tok_rows, model_width)
    reduced = (
        lax.psum_scatter(query_grad, "seq", scatter_dimension=0, tiled=True),
        lax.psum_scatter(key_grad, "seq", scatter_dimension=0, tiled=True),
        lax.psum_scatter(value_grad, "seq", scatter_dimension=0, tiled=True),
        lax.psum_scatter(gate_grad, "seq", scatter_dimension=0, tiled=True),
        lax.psum_scatter(out_grad, "seq", scatter_dimension=1, tiled=True),
        lax.psum_scatter(glu_grad, "seq", scatter_dimension=0, tiled=True),
        lax.psum_scatter(up_grad, "seq", scatter_dimension=0, tiled=True),
        lax.psum_scatter(down_grad, "seq", scatter_dimension=1, tiled=True),
        lax.psum_scatter(attngain_grad, "seq", scatter_dimension=0, tiled=True),
        lax.psum_scatter(ffngain_grad, "seq", scatter_dimension=0, tiled=True),
    )
    return (
        outputs,
        input_out,
        reduced[8],
        reduced[0],
        reduced[1],
        reduced[2],
        reduced[3],
        reduced[4],
        reduced[9],
        reduced[5],
        reduced[6],
        reduced[7],
    )


def solution(mesh):
    return jax.shard_map(
        on_device,
        mesh=mesh,
        in_specs=(
            P(None, "seq", None),
            P(None, "seq", None),
            P("seq"),
            P("seq", "tp"),
            P("seq", "tp"),
            P("seq", "tp"),
            P("seq", "tp"),
            P("tp", "seq"),
            P("seq"),
            P("seq", "tp"),
            P("seq", "tp"),
            P("tp", "seq"),
            P("tp"),
        ),
        out_specs=(
            P(None, "seq", None),
            P(None, "seq", None),
            P("seq"),
            P("seq", "tp"),
            P("seq", "tp"),
            P("seq", "tp"),
            P("seq", "tp"),
            P("tp", "seq"),
            P("seq"),
            P("seq", "tp"),
            P("seq", "tp"),
            P("tp", "seq"),
        ),
        check_vma=False,
    )
```

profile of v0, /device:TPU:0, one launch (start us, length us, event | category | flops | bytes accessed | tf_op | source)
XLA Modules:
  0.0 2463.8 jit_solution(17136700813776060130)
XLA Ops:
  66.0 45.9 %all-gather.15.cloned.1.call-done = bf16[2048,512]{1,0:T(8,128)(2,1)} async-done(((bf16[256,512]{1,0:T(8,128)(2,1)}), bf16[2048,512]{1,0:T(8,128)(2,1)}) %all-gather.15.cloned.1.call-update) | async-done | bytes 2097168 | tf_op jit(solution)/shard_map/all_gather | solution.py:194
  122.3 57.4 %all-gather.13.cloned.1.call-done = bf16[2048,864]{0,1:T(8,128)(2,1)} async-done(((bf16[256,864]{0,1:T(8,128)(2,1)}), bf16[2048,864]{0,1:T(8,128)(2,1)}) %all-gather.13.cloned.1.call-update) | async-done | bytes 3538960 | tf_op jit(solution)/shard_map/all_gather | solution.py:196
  186.6 373.1 %while.20 = (s32[]{:T(128)}, f32[2,2,256,432]{2,3,1,0:T(8,128)S(1)}, f32[2]{0:T(128)S(1)}, f32[2,2,256,432]{2,3,1,0:T(8,128)S(1)}, s32[]{:T(128)}) while((s32[]{:T(128)}, f32[2,2,256,432]{2,3,1,0:T(8,128)S(1)}, f32[2]{0:T(128)S(1)}, f32[2,2,256,432]{2,3,1,0:T(8,128)S(1)}, s32[]{:T(128)}) %tuple.65), condition=%wide.region_3.4_spmd, body=%wide.region_2.3_spmd.sunk | while | flops 884738 | bytes 12386413 | solution.py:164
  191.6 48.9 %collective-permute-done = f32[2,2,256,432]{2,3,1,0:T(8,128)S(1)} collective-permute-done((f32[2,2,256,432]{2,3,1,0:T(8,128)}, f32[2,2,256,432]{2,3,1,0:T(8,128)S(1)}, u32[]{:S(2)}, u32[]{:S(2)}) %collective-permute-start) | collective-permute-done | bytes 1769504 | tf_op jit(solution)/shard_map/while/body/eval_jaxpr/ppermute | solution.py:17
  265.2 42.4 %collective-permute-done = f32[2,2,256,432]{2,3,1,0:T(8,128)S(1)} collective-permute-done((f32[2,2,256,432]{2,3,1,0:T(8,128)}, f32[2,2,256,432]{2,3,1,0:T(8,128)S(1)}, u32[]{:S(2)}, u32[]{:S(2)}) %collective-permute-start) | collective-permute-done | bytes 1769504 | tf_op jit(solution)/shard_map/while/body/eval_jaxpr/ppermute | solution.py:17
  327.7 50.1 %collective-permute-done = f32[2,2,256,432]{2,3,1,0:T(8,128)S(1)} collective-permute-done((f32[2,2,256,432]{2,3,1,0:T(8,128)}, f32[2,2,256,432]{2,3,1,0:T(8,128)S(1)}, u32[]{:S(2)}, u32[]{:S(2)}) %collective-permute-start) | collective-permute-done | bytes 1769504 | tf_op jit(solution)/shard_map/while/body/eval_jaxpr/ppermute | solution.py:17
  601.9 65.3 %all-reduce.8.cloned.1.call-done = f32[512,2048]{1,0:T(8,128)} async-done(((f32[512,2048]{1,0:T(8,128)}), f32[512,2048]{1,0:T(8,128)}) %all-reduce.8.cloned.1.call-update) | async-done | bytes 4194320 | tf_op jit(solution)/shard_map/psum | solution.py:251
  674.6 62.0 %all-gather.21.cloned.1.call-done = bf16[2048,864]{0,1:T(8,128)(2,1)} async-done(((bf16[256,864]{0,1:T(8,128)(2,1)}), bf16[2048,864]{0,1:T(8,128)(2,1)}) %all-gather.21.cloned.1.call-update) | async-done | bytes 3538960 | tf_op jit(solution)/shard_map/all_gather | solution.py:199
  742.5 61.6 %all-gather.23.cloned.1.call-done = bf16[2048,864]{0,1:T(8,128)(2,1)} async-done(((bf16[256,864]{0,1:T(8,128)(2,1)}), bf16[2048,864]{0,1:T(8,128)(2,1)}) %all-gather.23.cloned.1.call-update) | async-done | bytes 3538960 | tf_op jit(solution)/shard_map/all_gather | solution.py:200
  809.9 61.5 %all-gather.25.cloned.1.call-done = bf16[864,2048]{1,0:T(8,128)(2,1)} async-done(((bf16[864,256]{1,0:T(8,128)(2,1)}), bf16[864,2048]{1,0:T(8,128)(2,1)}) %all-gather.25.cloned.1.call-update) | async-done | bytes 3538960 | tf_op jit(solution)/shard_map/all_gather | solution.py:201
  893.1 76.8 %all-reduce.10.cloned.1.call-done = f32[512,2048]{1,0:T(8,128)} async-done(((f32[512,2048]{1,0:T(8,128)}), f32[512,2048]{1,0:T(8,128)}) %all-reduce.10.cloned.1.call-update) | async-done | bytes 4194320 | tf_op jit(solution)/shard_map/psum | solution.py:293
  1001.3 293.0 %while.21 = (s32[]{:T(128)}, f32[2,2,256,432]{2,3,1,0:T(8,128)S(1)}, f32[2]{0:T(128)S(1)}, f32[2,2,256,432]{2,3,1,0:T(8,128)S(1)}, s32[]{:T(128)}) while((s32[]{:T(128)}, f32[2,2,256,432]{2,3,1,0:T(8,128)S(1)}, f32[2]{0:T(128)S(1)}, f32[2,2,256,432]{2,3,1,0:T(8,128)S(1)}, s32[]{:T(128)}) %tuple.110), condition=%wide.region_16.17_spmd, body=%wide.region_15.16_spmd.sunk | while | flops 884738 | bytes 12386413 | solution.py:172
  1004.1 40.8 %collective-permute-done.1 = f32[2,2,256,432]{2,3,1,0:T(8,128)S(1)} collective-permute-done((f32[2,2,256,432]{2,3,1,0:T(8,128)}, f32[2,2,256,432]{2,3,1,0:T(8,128)S(1)}, u32[]{:S(2)}, u32[]{:S(2)}) %collective-permute-start.1) | collective-permute-done | bytes 1769504 | tf_op jit(solution)/shard_map/while/body/eval_jaxpr/ppermute | solution.py:17
  1047.8 40.6 %collective-permute-done.1 = f32[2,2,256,432]{2,3,1,0:T(8,128)S(1)} collective-permute-done((f32[2,2,256,432]{2,3,1,0:T(8,128)}, f32[2,2,256,432]{2,3,1,0:T(8,128)S(1)}, u32[]{:S(2)}, u32[]{:S(2)}) %collective-permute-start.1) | collective-permute-done | bytes 1769504 | tf_op jit(solution)/shard_map/while/body/eval_jaxpr/ppermute | solution.py:17
  1091.2 40.0 %collective-permute-done.1 = f32[2,2,256,432]{2,3,1,0:T(8,128)S(1)} collective-permute-done((f32[2,2,256,432]{2,3,1,0:T(8,128)}, f32[2,2,256,432]{2,3,1,0:T(8,128)S(1)}, u32[]{:S(2)}, u32[]{:S(2)}) %collective-permute-start.1) | collective-permute-done | bytes 1769504 | tf_op jit(solution)/shard_map/while/body/eval_jaxpr/ppermute | solution.py:17
  1373.0 101.1 %all-reduce.12.cloned.1.call-done = (f32[512,2048]{1,0:T(8,128)}, f32[512,2048]{1,0:T(8,128)}) async-done(((f32[512,2048]{1,0:T(8,128)}, f32[512,2048]{1,0:T(8,128)}), (f32[512,2048]{1,0:T(8,128)}, f32[512,2048]{1,0:T(8,128)})) %all-reduce.12.cloned.1.call-update) | async-done | bytes 8388624 | tf_op jit(solution)/shard_map/psum | solution.py:259
  1527.2 39.8 %reduce-scatter.11.cloned.1.call-done = f32[256,512]{1,0:T(8,128)} async-done(((f32[2048,512]{1,0:T(8,128)}), f32[256,512]{1,0:T(8,128)}) %reduce-scatter.11.cloned.1.call-update) | async-done | bytes 524304 | tf_op jit(solution)/shard_map/reduce_scatter | solution.py:354
  1567.0 92.2 %reduce-scatter.9.cloned.1.call-done = f32[256,512]{1,0:T(8,128)} async-done(((f32[2048,512]{1,0:T(8,128)}), f32[256,512]{1,0:T(8,128)}) %reduce-scatter.9.cloned.1.call-update) | async-done | bytes 524304 | tf_op jit(solution)/shard_map/reduce_scatter | solution.py:353
  1659.2 133.3 %reduce-scatter.19.cloned.1.call-done = f32[256,864]{0,1:T(8,128)} async-done(((f32[2048,864]{0,1:T(8,128)}), f32[256,864]{0,1:T(8,128)}) %reduce-scatter.19.cloned.1.call-update) | async-done | bytes 884752 | tf_op jit(solution)/shard_map/reduce_scatter | solution.py:358
  1792.5 132.8 %reduce-scatter.21.cloned.1.call-done = f32[256,864]{0,1:T(8,128)} async-done(((f32[2048,864]{0,1:T(8,128)}), f32[256,864]{0,1:T(8,128)}) %reduce-scatter.21.cloned.1.call-update) | async-done | bytes 884752 | tf_op jit(solution)/shard_map/reduce_scatter | solution.py:359
  1925.3 132.8 %reduce-scatter.23.cloned.1.call-done = f32[864,256]{1,0:T(8,128)} async-done(((f32[864,2048]{1,0:T(8,128)}), f32[864,256]{1,0:T(8,128)}) %reduce-scatter.23.cloned.1.call-update) | async-done | bytes 884752 | tf_op jit(solution)/shard_map/reduce_scatter | solution.py:360
  2058.2 132.8 %reduce-scatter.17.cloned.1.call-done = f32[864,256]{1,0:T(8,128)} async-done(((f32[864,2048]{1,0:T(8,128)}), f32[864,256]{1,0:T(8,128)}) %reduce-scatter.17.cloned.1.call-update) | async-done | bytes 884752 | tf_op jit(solution)/shard_map/reduce_scatter | solution.py:357
  2191.0 132.8 %reduce-scatter.13.cloned.1.call-done = f32[256,864]{0,1:T(8,128)} async-done(((f32[2048,864]{0,1:T(8,128)}), f32[256,864]{0,1:T(8,128)}) %reduce-scatter.13.cloned.1.call-update) | async-done | bytes 884752 | tf_op jit(solution)/shard_map/reduce_scatter | solution.py:355
  2323.8 133.0 %reduce-scatter.15.cloned.1.call-done = f32[256,864]{0,1:T(8,128)} async-done(((f32[2048,864]{0,1:T(8,128)}), f32[256,864]{0,1:T(8,128)}) %reduce-scatter.15.cloned.1.call-update) | async-done | bytes 884752 | tf_op jit(solution)/shard_map/reduce_scatter | solution.py:356
  (319 shorter events, 722.8 us)
Async XLA Ops:
  7.2 54.9 %all-gather.17.cloned.1.call-start = ((), (), s32[]{:S(2)}) async-start(), calls=%async_computation.11 | async-start | bytes 2359296 | tf_op jit(solution)/shard_map/all_gather | solution.py:195
  7.9 103.9 %all-gather.15.cloned.1.call-start = ((), (), s32[]{:S(2)}) async-start(), calls=%async_computation.10 | async-start | bytes 2359296 | tf_op jit(solution)/shard_map/all_gather | solution.py:194
  8.7 171.0 %all-gather.13.cloned.1.call-start = ((), (), s32[]{:S(2)}) async-start(), calls=%async_computation.9 | async-start | bytes 3981312 | tf_op jit(solution)/shard_map/all_gather | solution.py:196
  9.4 556.9 %all-gather.11.cloned.1.call-start = ((), (), s32[]{:S(2)}) async-start(), calls=%async_computation.8 | async-start | bytes 3981312 | tf_op jit(solution)/shard_map/all_gather | solution.py:197
  10.0 563.2 %all-gather.19.cloned.1.call-start = ((), (), s32[]{:S(2)}) async-start(), calls=%async_computation.12 | async-start | bytes 3981312 | tf_op jit(solution)/shard_map/all_gather | solution.py:198
  10.6 656.7 %all-reduce.8.cloned.1.call-start = ((), (), s32[]{:S(2)}) async-start(), calls=%async_computation.13 | async-start | bytes 8388608 | tf_op jit(solution)/shard_map/psum | solution.py:251
  188.2 52.4 %collective-permute-start = (f32[2,2,256,432]{2,3,1,0:T(8,128)}, f32[2,2,256,432]{2,3,1,0:T(8,128)S(1)}, u32[]{:S(2)}, u32[]{:S(2)}) collective-permute-start(f32[2,2,256,432]{2,3,1,0:T(8,128)} %multiply_add_fusion.5), channel_id=1, source_target_pairs={{0,4},{4,8},{8,12},{12,16},{16,20},{20,24},{24,28},{1,5},{5,9},{9,... | collective-permute-start | bytes 5308424 | tf_op jit(solution)/shard_map/while/body/eval_jaxpr/ppermute | solution.py:17
  242.2 65.5 %collective-permute-start = (f32[2,2,256,432]{2,3,1,0:T(8,128)}, f32[2,2,256,432]{2,3,1,0:T(8,128)S(1)}, u32[]{:S(2)}, u32[]{:S(2)}) collective-permute-start(f32[2,2,256,432]{2,3,1,0:T(8,128)} %multiply_add_fusion.5), channel_id=1, source_target_pairs={{0,4},{4,8},{8,12},{12,16},{16,20},{20,24},{24,28},{1,5},{5,9},{9,... | collective-permute-start | bytes 5308424 | tf_op jit(solution)/shard_map/while/body/eval_jaxpr/ppermute | solution.py:17
  309.3 68.5 %collective-permute-start = (f32[2,2,256,432]{2,3,1,0:T(8,128)}, f32[2,2,256,432]{2,3,1,0:T(8,128)S(1)}, u32[]{:S(2)}, u32[]{:S(2)}) collective-permute-start(f32[2,2,256,432]{2,3,1,0:T(8,128)} %multiply_add_fusion.5), channel_id=1, source_target_pairs={{0,4},{4,8},{8,12},{12,16},{16,20},{20,24},{24,28},{1,5},{5,9},{9,... | collective-permute-start | bytes 5308424 | tf_op jit(solution)/shard_map/while/body/eval_jaxpr/ppermute | solution.py:17
  379.3 51.4 %collective-permute-start = (f32[2,2,256,432]{2,3,1,0:T(8,128)}, f32[2,2,256,432]{2,3,1,0:T(8,128)S(1)}, u32[]{:S(2)}, u32[]{:S(2)}) collective-permute-start(f32[2,2,256,432]{2,3,1,0:T(8,128)} %multiply_add_fusion.5), channel_id=1, source_target_pairs={{0,4},{4,8},{8,12},{12,16},{16,20},{20,24},{24,28},{1,5},{5,9},{9,... | collective-permute-start | bytes 5308424 | tf_op jit(solution)/shard_map/while/body/eval_jaxpr/ppermute | solution.py:17
  579.9 156.7 %all-gather.21.cloned.1.call-start = ((), (), s32[]{:S(2)}) async-start(), calls=%async_computation.14 | async-start | bytes 3981312 | tf_op jit(solution)/shard_map/all_gather | solution.py:199
  580.6 223.4 %all-gather.23.cloned.1.call-start = ((), (), s32[]{:S(2)}) async-start(), calls=%async_computation.15 | async-start | bytes 3981312 | tf_op jit(solution)/shard_map/all_gather | solution.py:200
  581.4 290.1 %all-gather.25.cloned.1.call-start = ((), (), s32[]{:S(2)}) async-start(), calls=%async_computation.16 | async-start | bytes 3981312 | tf_op jit(solution)/shard_map/all_gather | solution.py:201
  582.1 387.7 %all-reduce.10.cloned.1.call-start = ((), (), s32[]{:S(2)}) async-start(), calls=%async_computation.17 | async-start | bytes 8388608 | tf_op jit(solution)/shard_map/psum | solution.py:293
  886.0 588.0 %all-reduce.12.cloned.1.call-start = ((), (), s32[]{:S(2)}) async-start(), calls=%async_computation.26 | async-start | bytes 16777216 | tf_op jit(solution)/shard_map/psum | solution.py:259
  1002.8 42.1 %collective-permute-start.1 = (f32[2,2,256,432]{2,3,1,0:T(8,128)}, f32[2,2,256,432]{2,3,1,0:T(8,128)S(1)}, u32[]{:S(2)}, u32[]{:S(2)}) collective-permute-start(f32[2,2,256,432]{2,3,1,0:T(8,128)} %multiply_add_fusion.6), channel_id=1, source_target_pairs={{4,0},{8,4},{12,8},{16,12},{20,16},{24,20},{28,24},{5,1},{9,5},{13... | collective-permute-start | bytes 5308424 | tf_op jit(solution)/shard_map/while/body/eval_jaxpr/ppermute | solution.py:17
  1318.6 248.4 %reduce-scatter.11.cloned.1.call-start = ((), (), s32[]{:S(2)}) async-start(), calls=%async_computation.19 | async-start | bytes 4718592 | tf_op jit(solution)/shard_map/reduce_scatter | solution.py:354
  1323.5 335.7 %reduce-scatter.9.cloned.1.call-start = ((), (), s32[]{:S(2)}) async-start(), calls=%async_computation.18 | async-start | bytes 4718592 | tf_op jit(solution)/shard_map/reduce_scatter | solution.py:353
  1327.0 465.5 %reduce-scatter.19.cloned.1.call-start = ((), (), s32[]{:S(2)}) async-start(), calls=%async_computation.23 | async-start | bytes 7962624 | tf_op jit(solution)/shard_map/reduce_scatter | solution.py:358
  1334.6 590.7 %reduce-scatter.21.cloned.1.call-start = ((), (), s32[]{:S(2)}) async-start(), calls=%async_computation.24 | async-start | bytes 7962624 | tf_op jit(solution)/shard_map/reduce_scatter | solution.py:359
  1342.3 715.8 %reduce-scatter.23.cloned.1.call-start = ((), (), s32[]{:S(2)}) async-start(), calls=%async_computation.25 | async-start | bytes 7962624 | tf_op jit(solution)/shard_map/reduce_scatter | solution.py:360
  1350.1 840.9 %reduce-scatter.17.cloned.1.call-start = ((), (), s32[]{:S(2)}) async-start(), calls=%async_computation.22 | async-start | bytes 7962624 | tf_op jit(solution)/shard_map/reduce_scatter | solution.py:357
  1358.3 965.6 %reduce-scatter.13.cloned.1.call-start = ((), (), s32[]{:S(2)}) async-start(), calls=%async_computation.20 | async-start | bytes 7962624 | tf_op jit(solution)/shard_map/reduce_scatter | solution.py:355
  1364.4 1092.5 %reduce-scatter.15.cloned.1.call-start = ((), (), s32[]{:S(2)}) async-start(), calls=%async_computation.21 | async-start | bytes 7962624 | tf_op jit(solution)/shard_map/reduce_scatter | solution.py:356
  (77 other events, 2231.7 us)
Sparse Core Ops, SparseCore 0:
  10.1 51.9 all-gather.16
  64.2 47.6 all-gather.14
  113.9 65.6 all-gather.12
  181.6 92.4 all-gather.10
  276.0 88.9 all-gather.18
  580.0 87.2 all-reduce.7
  669.3 67.2 all-gather.20
  738.7 65.3 all-gather.22
  806.1 65.3 all-gather.24
  886.2 83.6 all-reduce.9
  1318.7 155.3 all-reduce.11
  1478.1 88.8 reduce-scatter.10
  1571.2 87.9 reduce-scatter.8
  1663.3 129.1 reduce-scatter.18
  1796.6 128.6 reduce-scatter.20
  1929.5 128.6 reduce-scatter.22
  2062.3 128.6 reduce-scatter.16
  2195.1 128.6 reduce-scatter.12
  2328.1 128.6 reduce-scatter.14
where the time goes:
time: 2470 us; the launch traced here: 2460 us
  waiting for transfers between devices  2050 us (83%)
  matrix products  132 us (5%)
  starting transfers between devices  85.1 us (3%)
  blocking collectives  80.6 us (3%)
  other arithmetic  62.5 us (3%)
  local copies, waits for them, and re-layouts  37.7 us (2%)
    ppermute x14, waiting for transfers between devices, passed_along(): return lax.ppermute(block, axis, route)  560 us
    reduce_scatter x1, waiting for transfers between devices, on_device(): lax.psum_scatter(glu_grad, 'seq', scatter_dimension=0, tiled=True)  133 us
    reduce_scatter x1, waiting for transfers between devices, on_device(): lax.psum_scatter(gate_grad, 'seq', scatter_dimension=0, tiled=True)  133 us
    reduce_scatter x1, waiting for transfers between devices, on_device(): lax.psum_scatter(value_grad, 'seq', scatter_dimension=0, tiled=True)  133 us
    reduce_scatter x1, waiting for transfers between devices, on_device(): lax.psum_scatter(down_grad, 'seq', scatter_dimension=1, tiled=True)  133 us
    reduce_scatter x1, waiting for transfers between devices, on_device(): lax.psum_scatter(out_grad, 'seq', scatter_dimension=1, tiled=True)  133 us
    reduce_scatter x1, waiting for transfers between devices, on_device(): lax.psum_scatter(up_grad, 'seq', scatter_dimension=0, tiled=True)  133 us
    psum x1, waiting for transfers between devices, on_device(): lax.psum(jnp.dot(hidden, full_down, preferred_element_type=jnp.float32),...  101 us
  transfers between devices with their start and end apart: 33, of which 31 were waited for; matrix products, arithmetic and copies ran while one was open for 5% of the time, Pallas kernels for 0%

commit v1 on v0

--- a/solution.py
+++ b/solution.py
@@ -3,6 +3,7 @@
 import jax.numpy as jnp
 from jax import lax
 from jax.sharding import PartitionSpec as P
+from jax.lax import all_gather
 
 KEY = 256
 VAL = 432
@@ -248,7 +249,9 @@
     gate_act, gate_slope = swish_parts(gate_lin)
     group_flat = group_normed.reshape(row_count, local_heads * VAL)
     mixed = (gate_act * group_flat).astype(jnp.bfloat16)
-    attn_out = lax.psum(jnp.dot(mixed, full_out, preferred_element_type=jnp.float32), "tp")
+    attn_out = jnp.sum(
+        all_gather(jnp.dot(mixed, full_out, preferred_element_type=jnp.float32), "tp"), axis=0
+    )
     middle = residual + attn_out
     normed_two, inv_two = normalize(middle, EPS_LAYER)
     ffn_in = (normed_two * full_ffn_gain.astype(jnp.float32)).astype(jnp.bfloat16)

time: 2470 us -> 2540 us (1.028)
  other arithmetic: 62.5 us -> 102 us
    all_gather x0 -> x1, waiting for transfers between devices: none -> 86 us  [on_device(): all_gather(jnp.dot(mixed, full_out, preferred_element_type=jnp.float32),...]
    psum x1 -> x0, waiting for transfers between devices: 65.3 us -> none  [on_device(): lax.psum(jnp.dot(mixed, full_out, preferred_element_type=jnp.float32), 'tp')]
  transfers between devices with their start and end apart: 33 -> 33, of which waited for: 31 -> 31; matrix products, arithmetic and copies ran while one was open for 5% -> 7% of each run, Pallas kernels for 0% -> 0%
where the time goes in v1:
time: 2540 us; the launch traced here: 2530 us
  waiting for transfers between devices  2040 us (80%)
  matrix products  146 us (6%)
  other arithmetic  102 us (4%)
  starting transfers between devices  101 us (4%)
  blocking collectives  85.2 us (3%)
  local copies, waits for them, and re-layouts  40.8 us (2%)
    ppermute x14, waiting for transfers between devices, passed_along(): return lax.ppermute(block, axis, route)  542 us
    reduce_scatter x1, waiting for transfers between devices, on_device(): lax.psum_scatter(glu_grad, 'seq', scatter_dimension=0, tiled=True)  133 us
    reduce_scatter x1, waiting for transfers between devices, on_device(): lax.psum_scatter(gate_grad, 'seq', scatter_dimension=0, tiled=True)  133 us
    reduce_scatter x1, waiting for transfers between devices, on_device(): lax.psum_scatter(down_grad, 'seq', scatter_dimension=1, tiled=True)  133 us
    reduce_scatter x1, waiting for transfers between devices, on_device(): lax.psum_scatter(value_grad, 'seq', scatter_dimension=0, tiled=True)  133 us
    reduce_scatter x1, waiting for transfers between devices, on_device(): lax.psum_scatter(out_grad, 'seq', scatter_dimension=1, tiled=True)  133 us
    reduce_scatter x1, waiting for transfers between devices, on_device(): lax.psum_scatter(up_grad, 'seq', scatter_dimension=0, tiled=True)  133 us
    ppermute x14, starting transfers between devices, passed_along(): return lax.ppermute(block, axis, route)  99.3 us
  transfers between devices with their start and end apart: 33, of which 31 were waited for; matrix products, arithmetic and copies ran while one was open for 7% of the time, Pallas kernels for 0%

profile of v1, /device:TPU:0, one launch (start us, length us, event | category | flops | bytes accessed | tf_op | source)
XLA Modules:
  0.0 2526.5 jit_solution(10184365343012352262)
XLA Ops:
  66.0 45.9 %all-gather.17.cloned.1.call-done = bf16[2048,512]{1,0:T(8,128)(2,1)} async-done(((bf16[256,512]{1,0:T(8,128)(2,1)}), bf16[2048,512]{1,0:T(8,128)(2,1)}) %all-gather.17.cloned.1.call-update) | async-done | bytes 2097168 | tf_op jit(solution)/shard_map/all_gather | solution.py:195
  124.1 55.5 %all-gather.15.cloned.1.call-done = bf16[2048,864]{0,1:T(8,128)(2,1)} async-done(((bf16[256,864]{0,1:T(8,128)(2,1)}), bf16[2048,864]{0,1:T(8,128)(2,1)}) %all-gather.15.cloned.1.call-update) | async-done | bytes 3538960 | tf_op jit(solution)/shard_map/all_gather | solution.py:197
  189.6 384.0 %while.20 = (s32[]{:T(128)}, f32[2,2,256,432]{2,3,1,0:T(8,128)}, f32[2]{0:T(128)S(1)}, f32[2,2,256,432]{2,3,1,0:T(8,128)}, s32[]{:T(128)}) while((s32[]{:T(128)}, f32[2,2,256,432]{2,3,1,0:T(8,128)}, f32[2]{0:T(128)S(1)}, f32[2,2,256,432]{2,3,1,0:T(8,128)}, s32[]{:T(128)}) %tuple.66), condition=%wide.region_3.4_spmd, body=%wide.region_2.3_spmd.sunk | while | flops 884738 | bytes 12386413 | solution.py:165
  197.7 53.6 %collective-permute-done = f32[2,2,256,432]{2,3,1,0:T(8,128)} collective-permute-done((f32[2,2,256,432]{2,3,1,0:T(8,128)}, f32[2,2,256,432]{2,3,1,0:T(8,128)}, u32[]{:S(2)}, u32[]{:S(2)}) %collective-permute-start) | collective-permute-done | bytes 1769504 | tf_op jit(solution)/shard_map/while/body/eval_jaxpr/ppermute | solution.py:18
  273.4 41.2 %collective-permute-done = f32[2,2,256,432]{2,3,1,0:T(8,128)} collective-permute-done((f32[2,2,256,432]{2,3,1,0:T(8,128)}, f32[2,2,256,432]{2,3,1,0:T(8,128)}, u32[]{:S(2)}, u32[]{:S(2)}) %collective-permute-start) | collective-permute-done | bytes 1769504 | tf_op jit(solution)/shard_map/while/body/eval_jaxpr/ppermute | solution.py:18
  622.1 86.0 %all-gather.29.cloned.1.call-done = f32[2048,2048]{1,0:T(8,128)} async-done(((f32[512,2048]{1,0:T(8,128)}), f32[2048,2048]{1,0:T(8,128)}) %all-gather.29.cloned.1.call-update) | async-done | bytes 16777232 | tf_op jit(solution)/shard_map/all_gather | solution.py:253
  724.9 52.4 %all-gather.23.cloned.1.call-done = bf16[2048,864]{0,1:T(8,128)(2,1)} async-done(((bf16[256,864]{0,1:T(8,128)(2,1)}), bf16[2048,864]{0,1:T(8,128)(2,1)}) %all-gather.23.cloned.1.call-update) | async-done | bytes 3538960 | tf_op jit(solution)/shard_map/all_gather | solution.py:200
  783.2 61.5 %all-gather.25.cloned.1.call-done = bf16[2048,864]{0,1:T(8,128)(2,1)} async-done(((bf16[256,864]{0,1:T(8,128)(2,1)}), bf16[2048,864]{0,1:T(8,128)(2,1)}) %all-gather.25.cloned.1.call-update) | async-done | bytes 3538960 | tf_op jit(solution)/shard_map/all_gather | solution.py:201
  850.6 61.5 %all-gather.27.cloned.1.call-done = bf16[864,2048]{1,0:T(8,128)(2,1)} async-done(((bf16[864,256]{1,0:T(8,128)(2,1)}), bf16[864,2048]{1,0:T(8,128)(2,1)}) %all-gather.27.cloned.1.call-update) | async-done | bytes 3538960 | tf_op jit(solution)/shard_map/all_gather | solution.py:202
  933.6 77.2 %all-reduce.7.cloned.1.call-done = f32[512,2048]{1,0:T(8,128)} async-done(((f32[512,2048]{1,0:T(8,128)}), f32[512,2048]{1,0:T(8,128)}) %all-reduce.7.cloned.1.call-update) | async-done | bytes 4194320 | tf_op jit(solution)/shard_map/psum | solution.py:296
  1046.9 307.6 %while.21 = (s32[]{:T(128)}, f32[2,2,256,432]{2,3,1,0:T(8,128)}, f32[2]{0:T(128)S(1)}, f32[2,2,256,432]{2,3,1,0:T(8,128)}, s32[]{:T(128)}) while((s32[]{:T(128)}, f32[2,2,256,432]{2,3,1,0:T(8,128)}, f32[2]{0:T(128)S(1)}, f32[2,2,256,432]{2,3,1,0:T(8,128)}, s32[]{:T(128)}) %tuple.111), condition=%wide.region_16.17_spmd, body=%wide.region_15.16_spmd.sunk | while | flops 884738 | bytes 12386413 | solution.py:173
  1051.7 40.9 %collective-permute-done.1 = f32[2,2,256,432]{2,3,1,0:T(8,128)} collective-permute-done((f32[2,2,256,432]{2,3,1,0:T(8,128)}, f32[2,2,256,432]{2,3,1,0:T(8,128)}, u32[]{:S(2)}, u32[]{:S(2)}) %collective-permute-start.1) | collective-permute-done | bytes 1769504 | tf_op jit(solution)/shard_map/while/body/eval_jaxpr/ppermute | solution.py:18
  1097.4 40.7 %collective-permute-done.1 = f32[2,2,256,432]{2,3,1,0:T(8,128)} collective-permute-done((f32[2,2,256,432]{2,3,1,0:T(8,128)}, f32[2,2,256,432]{2,3,1,0:T(8,128)}, u32[]{:S(2)}, u32[]{:S(2)}) %collective-permute-start.1) | collective-permute-done | bytes 1769504 | tf_op jit(solution)/shard_map/while/body/eval_jaxpr/ppermute | solution.py:18
  1143.0 40.1 %collective-permute-done.1 = f32[2,2,256,432]{2,3,1,0:T(8,128)} collective-permute-done((f32[2,2,256,432]{2,3,1,0:T(8,128)}, f32[2,2,256,432]{2,3,1,0:T(8,128)}, u32[]{:S(2)}, u32[]{:S(2)}) %collective-permute-start.1) | collective-permute-done | bytes 1769504 | tf_op jit(solution)/shard_map/while/body/eval_jaxpr/ppermute | solution.py:18
  1187.9 39.3 %collective-permute-done.1 = f32[2,2,256,432]{2,3,1,0:T(8,128)} collective-permute-done((f32[2,2,256,432]{2,3,1,0:T(8,128)}, f32[2,2,256,432]{2,3,1,0:T(8,128)}, u32[]{:S(2)}, u32[]{:S(2)}) %collective-permute-start.1) | collective-permute-done | bytes 1769504 | tf_op jit(solution)/shard_map/while/body/eval_jaxpr/ppermute | solution.py:18
  1441.0 95.9 %all-reduce.9.cloned.1.call-done = (f32[512,2048]{1,0:T(8,128)}, f32[512,2048]{1,0:T(8,128)}) async-done(((f32[512,2048]{1,0:T(8,128)}, f32[512,2048]{1,0:T(8,128)}), (f32[512,2048]{1,0:T(8,128)}, f32[512,2048]{1,0:T(8,128)})) %all-reduce.9.cloned.1.call-update) | async-done | bytes 8388624 | tf_op jit(solution)/shard_map/psum | solution.py:262
  1590.0 39.9 %reduce-scatter.11.cloned.1.call-done = f32[256,512]{1,0:T(8,128)} async-done(((f32[2048,512]{1,0:T(8,128)}), f32[256,512]{1,0:T(8,128)}) %reduce-scatter.11.cloned.1.call-update) | async-done | bytes 524304 | tf_op jit(solution)/shard_map/reduce_scatter | solution.py:357
  1629.9 92.2 %reduce-scatter.9.cloned.1.call-done = f32[256,512]{1,0:T(8,128)} async-done(((f32[2048,512]{1,0:T(8,128)}), f32[256,512]{1,0:T(8,128)}) %reduce-scatter.9.cloned.1.call-update) | async-done | bytes 524304 | tf_op jit(solution)/shard_map/reduce_scatter | solution.py:356
  1722.1 133.3 %reduce-scatter.19.cloned.1.call-done = f32[256,864]{0,1:T(8,128)} async-done(((f32[2048,864]{0,1:T(8,128)}), f32[256,864]{0,1:T(8,128)}) %reduce-scatter.19.cloned.1.call-update) | async-done | bytes 884752 | tf_op jit(solution)/shard_map/reduce_scatter | solution.py:361
  1855.4 132.8 %reduce-scatter.21.cloned.1.call-done = f32[256,864]{0,1:T(8,128)} async-done(((f32[2048,864]{0,1:T(8,128)}), f32[256,864]{0,1:T(8,128)}) %reduce-scatter.21.cloned.1.call-update) | async-done | bytes 884752 | tf_op jit(solution)/shard_map/reduce_scatter | solution.py:362
  1988.2 132.8 %reduce-scatter.23.cloned.1.call-done = f32[864,256]{1,0:T(8,128)} async-done(((f32[864,2048]{1,0:T(8,128)}), f32[864,256]{1,0:T(8,128)}) %reduce-scatter.23.cloned.1.call-update) | async-done | bytes 884752 | tf_op jit(solution)/shard_map/reduce_scatter | solution.py:363
  2121.0 132.8 %reduce-scatter.17.cloned.1.call-done = f32[864,256]{1,0:T(8,128)} async-done(((f32[864,2048]{1,0:T(8,128)}), f32[864,256]{1,0:T(8,128)}) %reduce-scatter.17.cloned.1.call-update) | async-done | bytes 884752 | tf_op jit(solution)/shard_map/reduce_scatter | solution.py:360
  2253.8 132.8 %reduce-scatter.13.cloned.1.call-done = f32[256,864]{0,1:T(8,128)} async-done(((f32[2048,864]{0,1:T(8,128)}), f32[256,864]{0,1:T(8,128)}) %reduce-scatter.13.cloned.1.call-update) | async-done | bytes 884752 | tf_op jit(solution)/shard_map/reduce_scatter | solution.py:358
  2386.6 133.0 %reduce-scatter.15.cloned.1.call-done = f32[256,864]{0,1:T(8,128)} async-done(((f32[2048,864]{0,1:T(8,128)}), f32[256,864]{0,1:T(8,128)}) %reduce-scatter.15.cloned.1.call-update) | async-done | bytes 884752 | tf_op jit(solution)/shard_map/reduce_scatter | solution.py:359
  (285 shorter events, 788.6 us)
Async XLA Ops:
  7.2 54.9 %all-gather.19.cloned.1.call-start = ((), (), s32[]{:S(2)}) async-start(), calls=%async_computation.11 | async-start | bytes 2359296 | tf_op jit(solution)/shard_map/all_gather | solution.py:196
  7.9 103.9 %all-gather.17.cloned.1.call-start = ((), (), s32[]{:S(2)}) async-start(), calls=%async_computation.10 | async-start | bytes 2359296 | tf_op jit(solution)/shard_map/all_gather | solution.py:195
  8.7 171.0 %all-gather.15.cloned.1.call-start = ((), (), s32[]{:S(2)}) async-start(), calls=%async_computation.9 | async-start | bytes 3981312 | tf_op jit(solution)/shard_map/all_gather | solution.py:197
  9.4 572.5 %all-gather.13.cloned.1.call-start = ((), (), s32[]{:S(2)}) async-start(), calls=%async_computation.8 | async-start | bytes 3981312 | tf_op jit(solution)/shard_map/all_gather | solution.py:198
  10.0 578.7 %all-gather.21.cloned.1.call-start = ((), (), s32[]{:S(2)}) async-start(), calls=%async_computation.12 | async-start | bytes 3981312 | tf_op jit(solution)/shard_map/all_gather | solution.py:199
  10.6 697.5 %all-gather.29.cloned.1.call-start = ((), (), s32[]{:S(2)}) async-start(), calls=%async_computation.25 | async-start | bytes 20971520 | tf_op jit(solution)/shard_map/all_gather | solution.py:253
  193.1 58.2 %collective-permute-start = (f32[2,2,256,432]{2,3,1,0:T(8,128)}, f32[2,2,256,432]{2,3,1,0:T(8,128)}, u32[]{:S(2)}, u32[]{:S(2)}) collective-permute-start(f32[2,2,256,432]{2,3,1,0:T(8,128)} %multiply_add_fusion.5), channel_id=1, source_target_pairs={{0,4},{4,8},{8,12},{12,16},{16,20},{20,24},{24,28},{1,5},{5,9},{9,... | collective-permute-start | bytes 5308424 | tf_op jit(solution)/shard_map/while/body/eval_jaxpr/ppermute | solution.py:18
  254.9 59.7 %collective-permute-start = (f32[2,2,256,432]{2,3,1,0:T(8,128)}, f32[2,2,256,432]{2,3,1,0:T(8,128)}, u32[]{:S(2)}, u32[]{:S(2)}) collective-permute-start(f32[2,2,256,432]{2,3,1,0:T(8,128)} %multiply_add_fusion.5), channel_id=1, source_target_pairs={{0,4},{4,8},{8,12},{12,16},{16,20},{20,24},{24,28},{1,5},{5,9},{9,... | collective-permute-start | bytes 5308424 | tf_op jit(solution)/shard_map/while/body/eval_jaxpr/ppermute | solution.py:18
  318.1 58.8 %collective-permute-start = (f32[2,2,256,432]{2,3,1,0:T(8,128)}, f32[2,2,256,432]{2,3,1,0:T(8,128)}, u32[]{:S(2)}, u32[]{:S(2)}) collective-permute-start(f32[2,2,256,432]{2,3,1,0:T(8,128)} %multiply_add_fusion.5), channel_id=1, source_target_pairs={{0,4},{4,8},{8,12},{12,16},{16,20},{20,24},{24,28},{1,5},{5,9},{9,... | collective-permute-start | bytes 5308424 | tf_op jit(solution)/shard_map/while/body/eval_jaxpr/ppermute | solution.py:18
  380.4 55.4 %collective-permute-start = (f32[2,2,256,432]{2,3,1,0:T(8,128)}, f32[2,2,256,432]{2,3,1,0:T(8,128)}, u32[]{:S(2)}, u32[]{:S(2)}) collective-permute-start(f32[2,2,256,432]{2,3,1,0:T(8,128)} %multiply_add_fusion.5), channel_id=1, source_target_pairs={{0,4},{4,8},{8,12},{12,16},{16,20},{20,24},{24,28},{1,5},{5,9},{9,... | collective-permute-start | bytes 5308424 | tf_op jit(solution)/shard_map/while/body/eval_jaxpr/ppermute | solution.py:18
  483.8 45.6 %collective-permute-start = (f32[2,2,256,432]{2,3,1,0:T(8,128)}, f32[2,2,256,432]{2,3,1,0:T(8,128)}, u32[]{:S(2)}, u32[]{:S(2)}) collective-permute-start(f32[2,2,256,432]{2,3,1,0:T(8,128)} %multiply_add_fusion.5), channel_id=1, source_target_pairs={{0,4},{4,8},{8,12},{12,16},{16,20},{20,24},{24,28},{1,5},{5,9},{9,... | collective-permute-start | bytes 5308424 | tf_op jit(solution)/shard_map/while/body/eval_jaxpr/ppermute | solution.py:18
  595.4 181.9 %all-gather.23.cloned.1.call-start = ((), (), s32[]{:S(2)}) async-start(), calls=%async_computation.13 | async-start | bytes 3981312 | tf_op jit(solution)/shard_map/all_gather | solution.py:200
  596.2 248.5 %all-gather.25.cloned.1.call-start = ((), (), s32[]{:S(2)}) async-start(), calls=%async_computation.14 | async-start | bytes 3981312 | tf_op jit(solution)/shard_map/all_gather | solution.py:201
  596.9 315.2 %all-gather.27.cloned.1.call-start = ((), (), s32[]{:S(2)}) async-start(), calls=%async_computation.15 | async-start | bytes 3981312 | tf_op jit(solution)/shard_map/all_gather | solution.py:202
  597.7 413.1 %all-reduce.7.cloned.1.call-start = ((), (), s32[]{:S(2)}) async-start(), calls=%async_computation.16 | async-start | bytes 8388608 | tf_op jit(solution)/shard_map/psum | solution.py:296
  926.9 610.0 %all-reduce.9.cloned.1.call-start = ((), (), s32[]{:S(2)}) async-start(), calls=%async_computation.26 | async-start | bytes 16777216 | tf_op jit(solution)/shard_map/psum | solution.py:262
  1381.4 248.4 %reduce-scatter.11.cloned.1.call-start = ((), (), s32[]{:S(2)}) async-start(), calls=%async_computation.18 | async-start | bytes 4718592 | tf_op jit(solution)/shard_map/reduce_scatter | solution.py:357
  1387.3 334.7 %reduce-scatter.9.cloned.1.call-start = ((), (), s32[]{:S(2)}) async-start(), calls=%async_computation.17 | async-start | bytes 4718592 | tf_op jit(solution)/shard_map/reduce_scatter | solution.py:356
  1392.4 463.0 %reduce-scatter.19.cloned.1.call-start = ((), (), s32[]{:S(2)}) async-start(), calls=%async_computation.22 | async-start | bytes 7962624 | tf_op jit(solution)/shard_map/reduce_scatter | solution.py:361
  1400.0 588.2 %reduce-scatter.21.cloned.1.call-start = ((), (), s32[]{:S(2)}) async-start(), calls=%async_computation.23 | async-start | bytes 7962624 | tf_op jit(solution)/shard_map/reduce_scatter | solution.py:362
  1407.7 713.3 %reduce-scatter.23.cloned.1.call-start = ((), (), s32[]{:S(2)}) async-start(), calls=%async_computation.24 | async-start | bytes 7962624 | tf_op jit(solution)/shard_map/reduce_scatter | solution.py:363
  1415.4 838.4 %reduce-scatter.17.cloned.1.call-start = ((), (), s32[]{:S(2)}) async-start(), calls=%async_computation.21 | async-start | bytes 7962624 | tf_op jit(solution)/shard_map/reduce_scatter | solution.py:360
  1423.8 962.8 %reduce-scatter.13.cloned.1.call-start = ((), (), s32[]{:S(2)}) async-start(), calls=%async_computation.19 | async-start | bytes 7962624 | tf_op jit(solution)/shard_map/reduce_scatter | solution.py:358
  1431.5 1088.1 %reduce-scatter.15.cloned.1.call-start = ((), (), s32[]{:S(2)}) async-start(), calls=%async_computation.20 | async-start | bytes 7962624 | tf_op jit(solution)/shard_map/reduce_scatter | solution.py:359
  (59 other events, 976.6 us)
Sparse Core Ops, SparseCore 0:
  10.1 51.9 all-gather.18
  64.2 47.6 all-gather.16
  113.9 65.6 all-gather.14
  181.5 89.0 all-gather.12
  272.5 91.7 all-gather.20
  595.5 112.4 all-gather.28
  710.1 67.1 all-gather.22
  779.3 65.3 all-gather.24
  846.8 65.3 all-gather.26
  927.0 83.6 all-reduce.6
  1381.6 155.2 all-reduce.8
  1541.0 88.8 reduce-scatter.10
  1634.1 87.9 reduce-scatter.8
  1726.2 129.1 reduce-scatter.18
  1859.5 128.6 reduce-scatter.20
  1992.3 128.6 reduce-scatter.22
  2125.1 128.6 reduce-scatter.16
  2257.9 128.6 reduce-scatter.12
  2390.9 128.6 reduce-scatter.14
